TPU v7x, 256 devices: a whole 4x4x8 slice. The times are simulated.
256 devices in a mesh: ep: 8 (over y, core), fsdp: 32 (over z, x).
Axes of the slice: x: 4, y: 4, z: 8, core: 2. Of those that a mesh axis runs over, the one named last changes fastest.
Arguments:
- w_down: float32 [16, 6400, 4096], P('ep', None, 'fsdp'), may hold values from -0.15625 to 0.15625
- router_weight: float32 [4096, 16], P('fsdp', 'ep'), may hold values from -0.09375 to 0.09375
- router_gain: float32 [4096], P('fsdp'), may hold values from 0.25 to 1.75
Outputs:
- serve_down: bfloat16 [16, 6400, 4096], P('ep', 'fsdp')
- scale_down: float32 [16, 6400], P('ep', 'fsdp')
- serve_router: bfloat16 [4096, 16], replicated
All inputs are finite; a program needn't handle non-finite values.
Results may differ from a plain program's by a relative error of at most 0.001.
Values may be sent and summed in bfloat16 or wider, within the bound.
A program may use at most 64 MiB of HBM per device.

v0:
```python
import jax
import jax.numpy as jnp
from jax import lax
from jax.sharding import Mesh
from jax.sharding import PartitionSpec as P

FSDP = ("fsdp_0", "fsdp_1")


def by_axis(array, axes):
    for axis in axes:
        array = lax.psum(array, axis)
    return array


def in_order(parts, dim):
    lengths = list(parts.shape[1:])
    lengths[dim] *= parts.shape[0]
    return jnp.moveaxis(parts, 0, dim).reshape(lengths)


def copy_for_each(array, axis):
    size = lax.axis_size(axis)
    return lax.all_to_all(
        jnp.broadcast_to(array[None], (size, *array.shape)), axis, 0, 0, tiled=True
    )


def gather_directly(array, axis, dim):
    return in_order(copy_for_each(array, axis), dim)


def body(w_down, router_weight, router_gain):
    total_down = by_axis(jnp.sum(w_down * w_down, axis=2), FSDP)
    scale_down = jnp.sqrt(total_down)
    narrow_down = (w_down / jnp.expand_dims(scale_down, 2)).astype(jnp.bfloat16)
    serve_down = lax.all_to_all(narrow_down, FSDP, split_axis=1, concat_axis=2, tiled=True)
    scale_down = lax.dynamic_slice_in_dim(
        scale_down, lax.axis_index(FSDP) * serve_down.shape[1], serve_down.shape[1], axis=1
    )
    part_router = (router_weight * router_gain[:, None]).astype(jnp.bfloat16)
    row_router = gather_directly(part_router, FSDP, 0)
    serve_router = lax.all_gather(row_router, "ep", axis=1, tiled=True)
    return (serve_down, scale_down, serve_router)


def solution(mesh):
    split = Mesh(mesh.devices.reshape(mesh.shape["ep"], 8, 4), ("ep", "fsdp_0", "fsdp_1"))
    return jax.shard_map(
        body,
        mesh=split,
        in_specs=(P("ep", None, FSDP), P(FSDP, "ep"), P(FSDP)),
        out_specs=(P("ep", FSDP, None), P("ep", FSDP), P()),
        check_vma=False,
    )
```

profile of v0, /device:TPU:8, one launch (start us, length us, event | category | flops | bytes accessed | tf_op | source)
XLA Modules:
  0.0 177.8 jit_solution(15432574918795712005)
XLA Ops:
  0.6 0.7 multiply_convert_fusion
  1.3 0.6 broadcast_in_dim.2
  1.9 11.3 %all-to-all-start.1 = ((bf16[32,128,2]{1,2,0:T(2,128)(2,1)}), bf16[32,128,2]{1,2,0:T(2,128)(2,1)S(1)}, u32[]{:S(2)}, u32[]{:S(2)}) async-start(bf16[32,128,2]{1,2,0:T(2,128)(2,1)} %broadcast_in_dim.2), calls=%async_computation.1 | async-start | bytes 32768 | tf_op jit(solution)/shard_map/all_to_all | solution.py:24
  13.3 4.6 %multiply_reduce_fusion = f32[2,6400]{1,0:T(2,128)S(1)} fusion(f32[2,6400,128]{2,1,0:T(8,128)} %param.3), kind=kLoop, calls=%fused_computation.1 | loop fusion | flops 3264000 | bytes 6604800 | tf_op jit(solution)/shard_map/reduce_sum | solution.py:34
  17.9 30.5 %psum.14 = f32[2,6400]{1,0:T(2,128)S(1)} all-reduce(f32[2,6400]{1,0:T(2,128)S(1)} %multiply_reduce_fusion), channel_id=1, replica_groups=mesh['ep'=8,'fsdp_0'=8,'fsdp_1'=4] {'fsdp_0'}, use_global_device_ids=true, to_apply=%region_1.0 | all-reduce | flops 12800 | bytes 102400 | tf_op jit(solution)/shard_map/psum | solution.py:12
  48.4 17.4 %psum.15 = f32[2,6400]{1,0:T(2,128)S(1)} all-reduce(f32[2,6400]{1,0:T(2,128)S(1)} %psum.14), channel_id=1, replica_groups=mesh['ep'=8,'fsdp_0'=8,'fsdp_1'=4] {'fsdp_1'}, use_global_device_ids=true, to_apply=%region_2.0 | all-reduce | flops 12800 | bytes 102400 | tf_op jit(solution)/shard_map/psum | solution.py:12
  65.8 0.1 sqrt.3
  65.9 4.7 %divide_convert_fusion = bf16[2,6400,128]{2,1,0:T(8,128)(2,1)S(1)} fusion(f32[2,6400,128]{2,1,0:T(8,128)} %param.3, f32[2,6400]{1,0:T(2,128)S(1)} %sqrt.3), kind=kLoop, calls=%fused_computation | loop fusion | flops 3276800 | bytes 9881600 | tf_op jit(solution)/shard_map/convert_element_type | solution.py:36
  70.6 27.9 %copy.10 = bf16[2,6400,128]{2,0,1:T(2,128)(2,1)} copy(bf16[2,6400,128]{2,1,0:T(8,128)(2,1)S(1)} %divide_convert_fusion) | data formatting | bytes 6553600 | tf_op jit(solution)/shard_map/convert_element_type | solution.py:36
  98.5 0.0 all-to-all-done.1
  98.5 5.7 %all-to-all-start = ((bf16[2,6400,128]{2,0,1:T(2,128)(2,1)}), bf16[2,6400,128]{2,0,1:T(2,128)(2,1)S(1)}, u32[]{:S(2)}, u32[]{:S(2)}) async-start(bf16[2,6400,128]{2,0,1:T(2,128)(2,1)} %copy.10), calls=%async_computation | async-start | bytes 6553600 | tf_op jit(solution)/shard_map/all_to_all | solution.py:37
  104.2 0.7 constant_dynamic-slice_fusion
  104.9 12.9 %all-gather = bf16[8,2,4096]{2,1,0:T(2,128)(2,1)S(1)} all-gather(bf16[1,2,4096]{2,1,0:T(2,128)(2,1)S(1)} %bitcast.13), channel_id=1, replica_groups=mesh['ep'=8,'fsdp_0'=8,'fsdp_1'=4] {'ep'}, dimensions={0}, use_global_device_ids=true | all-gather | bytes 147456 | tf_op jit(solution)/shard_map/all_gather | solution.py:43
  117.8 0.7 reshape.14
  118.5 50.5 %all-to-all-done = bf16[2,6400,128]{2,0,1:T(2,128)(2,1)S(1)} async-done(((bf16[2,6400,128]{2,0,1:T(2,128)(2,1)}), bf16[2,6400,128]{2,0,1:T(2,128)(2,1)S(1)}, u32[]{:S(2)}, u32[]{:S(2)}) %all-to-all-start) | async-done | bytes 3276832 | tf_op jit(solution)/shard_map/all_to_all | solution.py:37
  169.1 2.5 %copy.11 = bf16[2,200,32,128]{3,2,1,0:T(8,128)(2,1)} copy(bf16[2,200,32,128]{3,0,1,2:T(2,128)(2,1)S(1)} %bitcast.11) | data formatting | bytes 6553600 | tf_op jit(solution)/shard_map/all_to_all | solution.py:37
  171.6 6.2 %all_to_all.19 = bf16[2,200,4096]{2,1,0:T(8,128)(2,1)} reshape(bf16[2,200,32,128]{3,2,1,0:T(8,128)(2,1)} %copy.11) | data formatting | bytes 6553600 | tf_op jit(solution)/shard_map/all_to_all | solution.py:37
Async XLA Ops:
  1.9 96.6 %all-to-all-start.1 = ((bf16[32,128,2]{1,2,0:T(2,128)(2,1)}), bf16[32,128,2]{1,2,0:T(2,128)(2,1)S(1)}, u32[]{:S(2)}, u32[]{:S(2)}) async-start(bf16[32,128,2]{1,2,0:T(2,128)(2,1)} %broadcast_in_dim.2), calls=%async_computation.1 | async-start | bytes 32768 | tf_op jit(solution)/shard_map/all_to_all | solution.py:24
  98.5 70.6 %all-to-all-start = ((bf16[2,6400,128]{2,0,1:T(2,128)(2,1)}), bf16[2,6400,128]{2,0,1:T(2,128)(2,1)S(1)}, u32[]{:S(2)}, u32[]{:S(2)}) async-start(bf16[2,6400,128]{2,0,1:T(2,128)(2,1)} %copy.10), calls=%async_computation | async-start | bytes 6553600 | tf_op jit(solution)/shard_map/all_to_all | solution.py:37
where the time goes:
time: 178 us
  blocking collectives  60.9 us (34%)
  waiting for transfers between devices  50.5 us (28%)
  local copies, waits for them, and re-layouts  38.6 us (22%)
  starting transfers between devices  17 us (10%)
  other arithmetic  10 us (6%)
    all_to_all x1, waiting for transfers between devices, body(): lax.all_to_all(narrow_down, FSDP, split_axis=1, concat_axis=2, tiled=True)  50.5 us
    psum x2, blocking collectives, by_axis(): array = lax.psum(array, axis)  47.9 us
    convert_element_type x1, local copies, waits for them, and re-layouts, body(): narrow_down = (w_down / jnp.expand_dims(scale_down, 2)).astype(jnp.bfloat16)  27.9 us
    all_gather x1, blocking collectives, body(): serve_router = lax.all_gather(row_router, 'ep', axis=1, tiled=True)  12.9 us
    all_to_all x1, starting transfers between devices, copy_for_each(): lax.all_to_all(jnp.broadcast_to(array[None], (size, *array.shape)), axis,...  11.3 us
    all_to_all x2, local copies, waits for them, and re-layouts, body(): lax.all_to_all(narrow_down, FSDP, split_axis=1, concat_axis=2, tiled=True)  8.73 us
    all_to_all x1, starting transfers between devices, body(): lax.all_to_all(narrow_down, FSDP, split_axis=1, concat_axis=2, tiled=True)  5.7 us
    convert_element_type x1, other arithmetic, body(): narrow_down = (w_down / jnp.expand_dims(scale_down, 2)).astype(jnp.bfloat16)  4.71 us
  transfers between devices with their start and end apart: 2, of which 1 were waited for; matrix products, arithmetic and copies ran while one was open for 22% of the time, Pallas kernels for 0%

commit v1 on v0

--- a/solution.py
+++ b/solution.py
@@ -5,6 +5,19 @@
 from jax.sharding import PartitionSpec as P
 
 FSDP = ("fsdp_0", "fsdp_1")
+
+
+def gather_around(x, axis, dim):
+    ways = lax.axis_size(axis)
+    up = [(d, (d + 1) % ways) for d in range(ways)]
+    down = [(d, (d - 1) % ways) for d in range(ways)]
+    earlier, later = ([x], [x])
+    for _ in range(ways // 2):
+        earlier.append(lax.ppermute(earlier[-1], axis, up))
+    for _ in range((ways - 1) // 2):
+        later.append(lax.ppermute(later[-1], axis, down))
+    line = jnp.concatenate([*earlier[::-1], *later[1:]], axis=dim)
+    return jnp.roll(line, (lax.axis_index(axis) - ways // 2) * x.shape[dim], axis=dim)
 
 
 def by_axis(array, axes):
@@ -40,7 +53,7 @@
     )
     part_router = (router_weight * router_gain[:, None]).astype(jnp.bfloat16)
     row_router = gather_directly(part_router, FSDP, 0)
-    serve_router = lax.all_gather(row_router, "ep", axis=1, tiled=True)
+    serve_router = gather_around(row_router, "ep", 1)
     return (serve_down, scale_down, serve_router)
 
 

time: 178 us -> 179 us (level)
  blocking collectives: 60.9 us -> 47.9 us
  starting transfers between devices: 17 us -> 22.2 us
  local copies, waits for them, and re-layouts: 38.6 us -> 43.2 us
  waiting for transfers between devices: 50.5 us -> 53.6 us
    all_gather x1 -> x0, blocking collectives: 12.9 us -> none  [body(): serve_router = lax.all_gather(row_router, 'ep', axis=1, tiled=True)]
    ppermute x0 -> x7, waiting for transfers between devices: none -> 5.68 us  [the longest x4 5.34 us: gather_around(): earlier.append(lax.ppermute(earlier[-1], axis, up))]
    ppermute x0 -> x7, starting transfers between devices: none -> 5.21 us  [the longest x3 5.18 us: gather_around(): later.append(lax.ppermute(later[-1], axis, down))]
    concatenate x0 -> x1, local copies, waits for them, and re-layouts: none -> 3.41 us  [gather_around(): jnp.roll(line, (lax.axis_index(axis) - ways // 2) * x.shape[dim], axis=dim)]
    all_to_all x1, waiting for transfers between devices: 50.5 us -> 48 us  [body(): lax.all_to_all(narrow_down, FSDP, split_axis=1, concat_axis=2, tiled=True)]
  transfers between devices with their start and end apart: 2 -> 9, of which waited for: 1 -> 6; matrix products, arithmetic and copies ran while one was open for 22% -> 24% of each run, Pallas kernels for 0% -> 0%
where the time goes in v1:
time: 179 us; the launch traced here: 178 us
  waiting for transfers between devices  53.6 us (30%)
  blocking collectives  47.9 us (27%)
  local copies, waits for them, and re-layouts  43.2 us (24%)
  starting transfers between devices  22.2 us (12%)
  other arithmetic  10 us (6%)
    all_to_all x1, waiting for transfers between devices, body(): lax.all_to_all(narrow_down, FSDP, split_axis=1, concat_axis=2, tiled=True)  48 us
    psum x2, blocking collectives, by_axis(): array = lax.psum(array, axis)  47.9 us
    convert_element_type x1, local copies, waits for them, and re-layouts, body(): narrow_down = (w_down / jnp.expand_dims(scale_down, 2)).astype(jnp.bfloat16)  27.9 us
    all_to_all x1, starting transfers between devices, copy_for_each(): lax.all_to_all(jnp.broadcast_to(array[None], (size, *array.shape)), axis,...  11.3 us
    all_to_all x2, local copies, waits for them, and re-layouts, body(): lax.all_to_all(narrow_down, FSDP, split_axis=1, concat_axis=2, tiled=True)  8.74 us
    all_to_all x1, starting transfers between devices, body(): lax.all_to_all(narrow_down, FSDP, split_axis=1, concat_axis=2, tiled=True)  5.7 us
    ppermute x4, waiting for transfers between devices, gather_around(): earlier.append(lax.ppermute(earlier[-1], axis, up))  5.34 us
    ppermute x3, starting transfers between devices, gather_around(): later.append(lax.ppermute(later[-1], axis, down))  5.18 us
  transfers between devices with their start and end apart: 9, of which 6 were waited for; matrix products, arithmetic and copies ran while one was open for 24% of the time, Pallas kernels for 0%

profile of v1, /device:TPU:8, one launch (start us, length us, event | category | flops | bytes accessed | tf_op | source)
XLA Modules:
  0.0 177.8 jit_solution(1075704525552873363)
XLA Ops:
  0.6 0.7 multiply_convert_fusion
  1.3 0.6 broadcast_in_dim.2
  1.9 11.3 %all-to-all-start.1 = ((bf16[32,128,2]{1,2,0:T(2,128)(2,1)}), bf16[32,128,2]{1,2,0:T(2,128)(2,1)S(1)}, u32[]{:S(2)}, u32[]{:S(2)}) async-start(bf16[32,128,2]{1,2,0:T(2,128)(2,1)} %broadcast_in_dim.2), calls=%async_computation.1 | async-start | bytes 32768 | tf_op jit(solution)/shard_map/all_to_all | solution.py:37
  13.3 4.6 %multiply_reduce_fusion = f32[2,6400]{1,0:T(2,128)S(1)} fusion(f32[2,6400,128]{2,1,0:T(8,128)} %param.3), kind=kLoop, calls=%fused_computation.1 | loop fusion | flops 3264000 | bytes 6604800 | tf_op jit(solution)/shard_map/reduce_sum | solution.py:47
  17.9 30.5 %psum.14 = f32[2,6400]{1,0:T(2,128)S(1)} all-reduce(f32[2,6400]{1,0:T(2,128)S(1)} %multiply_reduce_fusion), channel_id=1, replica_groups=mesh['ep'=8,'fsdp_0'=8,'fsdp_1'=4] {'fsdp_0'}, use_global_device_ids=true, to_apply=%region_1.0 | all-reduce | flops 12800 | bytes 102400 | tf_op jit(solution)/shard_map/psum | solution.py:25
  48.4 17.4 %psum.15 = f32[2,6400]{1,0:T(2,128)S(1)} all-reduce(f32[2,6400]{1,0:T(2,128)S(1)} %psum.14), channel_id=1, replica_groups=mesh['ep'=8,'fsdp_0'=8,'fsdp_1'=4] {'fsdp_1'}, use_global_device_ids=true, to_apply=%region_2.0 | all-reduce | flops 12800 | bytes 102400 | tf_op jit(solution)/shard_map/psum | solution.py:25
  65.8 0.1 sqrt.3
  65.9 4.7 %divide_convert_fusion = bf16[2,6400,128]{2,1,0:T(8,128)(2,1)S(1)} fusion(f32[2,6400,128]{2,1,0:T(8,128)} %param.3, f32[2,6400]{1,0:T(2,128)S(1)} %sqrt.3), kind=kLoop, calls=%fused_computation | loop fusion | flops 3276800 | bytes 9881600 | tf_op jit(solution)/shard_map/convert_element_type | solution.py:49
  70.6 27.9 %copy.10 = bf16[2,6400,128]{2,0,1:T(2,128)(2,1)} copy(bf16[2,6400,128]{2,1,0:T(8,128)(2,1)S(1)} %divide_convert_fusion) | data formatting | bytes 6553600 | tf_op jit(solution)/shard_map/convert_element_type | solution.py:49
  98.5 0.0 all-to-all-done.1
  98.5 5.7 %all-to-all-start = ((bf16[2,6400,128]{2,0,1:T(2,128)(2,1)}), bf16[2,6400,128]{2,0,1:T(2,128)(2,1)S(1)}, u32[]{:S(2)}, u32[]{:S(2)}) async-start(bf16[2,6400,128]{2,0,1:T(2,128)(2,1)} %copy.10), calls=%async_computation | async-start | bytes 6553600 | tf_op jit(solution)/shard_map/all_to_all | solution.py:50
  104.2 0.0 collective-permute-start
  104.2 1.7 collective-permute-start.4
  106.0 1.4 collective-permute-done
  107.4 0.0 collective-permute-start.1
  107.4 0.0 collective-permute-done.4
  107.4 0.6 copy-done
  108.0 1.4 collective-permute-start.5
  109.4 1.1 collective-permute-done.1
  110.6 0.0 collective-permute-start.2
  110.6 0.3 collective-permute-done.5
  110.9 2.0 %collective-permute-start.6 = (bf16[4096,2]{0,1:T(2,128)(2,1)S(1)}, bf16[4096,2]{0,1:T(2,128)(2,1)S(1)}, u32[]{:S(2)}, u32[]{:S(2)}) collective-permute-start(bf16[4096,2]{0,1:T(2,128)(2,1)S(1)} %collective-permute-done.5), channel_id=1, source_target_pairs={{0,224},{32,0},{64,32},{96,64},{128,96},{160,128},{192,160},{224,1... | collective-permute-start | bytes 49160 | tf_op jit(solution)/shard_map/ppermute | solution.py:18
  112.9 0.8 collective-permute-done.2
  113.7 0.0 collective-permute-start.3
  113.7 0.7 constant_dynamic-slice_fusion.1
  114.4 0.6 copy-done.5
  115.0 2.0 %collective-permute-done.3 = bf16[4096,2]{0,1:T(2,128)(2,1)} collective-permute-done((bf16[4096,2]{0,1:T(2,128)(2,1)S(1)}, bf16[4096,2]{0,1:T(2,128)(2,1)}, u32[]{:S(2)}, u32[]{:S(2)}) %collective-permute-start.3) | collective-permute-done | bytes 16416 | tf_op jit(solution)/shard_map/ppermute | solution.py:16
  117.0 3.4 %concatenate.6 = bf16[4096,32]{0,1:T(8,128)(2,1)S(1)} concatenate(bf16[4096,2]{0,1:T(2,128)(2,1)} %collective-permute-done.3, bf16[4096,2]{0,1:T(2,128)(2,1)} %copy-done.4, bf16[4096,2]{0,1:T(2,128)(2,1)} %copy-done.2, bf16[4096,2]{0,1:T(2,128)(2,1)} %copy-done, bf16[4096,2]{0,1:T(2,128)(2,1)S(1)} %bitcast.9, bf16[4096,2]{0,1:T(2,128)(2,1)} %copy-done.1, ...), dimensions={1} | concatenate | bytes 524288 | tf_op jit(solution)/shard_map/jit(_roll_dynamic)/concatenate | solution.py:20
  120.4 0.7 constant_dynamic-slice_fusion
  121.1 48.0 %all-to-all-done = bf16[2,6400,128]{2,0,1:T(2,128)(2,1)S(1)} async-done(((bf16[2,6400,128]{2,0,1:T(2,128)(2,1)}), bf16[2,6400,128]{2,0,1:T(2,128)(2,1)S(1)}, u32[]{:S(2)}, u32[]{:S(2)}) %all-to-all-start) | async-done | bytes 3276832 | tf_op jit(solution)/shard_map/all_to_all | solution.py:50
  169.1 2.5 %copy.11 = bf16[2,200,32,128]{3,2,1,0:T(8,128)(2,1)} copy(bf16[2,200,32,128]{3,0,1,2:T(2,128)(2,1)S(1)} %bitcast.6) | data formatting | bytes 6553600 | tf_op jit(solution)/shard_map/all_to_all | solution.py:50
  171.6 6.2 %all_to_all.19 = bf16[2,200,4096]{2,1,0:T(8,128)(2,1)} reshape(bf16[2,200,32,128]{3,2,1,0:T(8,128)(2,1)} %copy.11) | data formatting | bytes 6553600 | tf_op jit(solution)/shard_map/all_to_all | solution.py:50
  (11 shorter events, 0.0 us)
Async XLA Ops:
  1.9 96.6 %all-to-all-start.1 = ((bf16[32,128,2]{1,2,0:T(2,128)(2,1)}), bf16[32,128,2]{1,2,0:T(2,128)(2,1)S(1)}, u32[]{:S(2)}, u32[]{:S(2)}) async-start(bf16[32,128,2]{1,2,0:T(2,128)(2,1)} %broadcast_in_dim.2), calls=%async_computation.1 | async-start | bytes 32768 | tf_op jit(solution)/shard_map/all_to_all | solution.py:37
  98.5 70.6 %all-to-all-start = ((bf16[2,6400,128]{2,0,1:T(2,128)(2,1)}), bf16[2,6400,128]{2,0,1:T(2,128)(2,1)S(1)}, u32[]{:S(2)}, u32[]{:S(2)}) async-start(bf16[2,6400,128]{2,0,1:T(2,128)(2,1)} %copy.10), calls=%async_computation | async-start | bytes 6553600 | tf_op jit(solution)/shard_map/all_to_all | solution.py:50
  104.2 3.2 %collective-permute-start = (bf16[4096,2]{0,1:T(2,128)(2,1)S(1)}, bf16[4096,2]{0,1:T(2,128)(2,1)S(1)}, u32[]{:S(2)}, u32[]{:S(2)}) collective-permute-start(bf16[4096,2]{0,1:T(2,128)(2,1)S(1)} %bitcast.7), channel_id=1, source_target_pairs={{0,32},{32,64},{64,96},{96,128},{128,160},{160,192},{192,224},{224... | collective-permute-start | bytes 49160 | tf_op jit(solution)/shard_map/ppermute | solution.py:16
  104.2 3.2 %collective-permute-start.4 = (bf16[4096,2]{0,1:T(2,128)(2,1)S(1)}, bf16[4096,2]{0,1:T(2,128)(2,1)S(1)}, u32[]{:S(2)}, u32[]{:S(2)}) collective-permute-start(bf16[4096,2]{0,1:T(2,128)(2,1)S(1)} %bitcast.8), channel_id=1, source_target_pairs={{0,224},{32,0},{64,32},{96,64},{128,96},{160,128},{192,160},{224,1... | collective-permute-start | bytes 49160 | tf_op jit(solution)/shard_map/ppermute | solution.py:18
  107.4 0.6 copy-start
  107.4 3.2 %collective-permute-start.1 = (bf16[4096,2]{0,1:T(2,128)(2,1)S(1)}, bf16[4096,2]{0,1:T(2,128)(2,1)S(1)}, u32[]{:S(2)}, u32[]{:S(2)}) collective-permute-start(bf16[4096,2]{0,1:T(2,128)(2,1)S(1)} %collective-permute-done), channel_id=1, source_target_pairs={{0,32},{32,64},{64,96},{96,128},{128,160},{160,192},{192,224},{224... | collective-permute-start | bytes 49160 | tf_op jit(solution)/shard_map/ppermute | solution.py:16
  108.0 6.4 %copy-start.1 = (bf16[4096,2]{0,1:T(2,128)(2,1)}, bf16[4096,2]{0,1:T(2,128)(2,1)S(1)}, u32[]{:S(2)}) copy-start(bf16[4096,2]{0,1:T(2,128)(2,1)S(1)} %collective-permute-done.4) | copy-start | bytes 49156
  108.0 2.9 %collective-permute-start.5 = (bf16[4096,2]{0,1:T(2,128)(2,1)S(1)}, bf16[4096,2]{0,1:T(2,128)(2,1)S(1)}, u32[]{:S(2)}, u32[]{:S(2)}) collective-permute-start(bf16[4096,2]{0,1:T(2,128)(2,1)S(1)} %collective-permute-done.4), channel_id=1, source_target_pairs={{0,224},{32,0},{64,32},{96,64},{128,96},{160,128},{192,160},{224,1... | collective-permute-start | bytes 49160 | tf_op jit(solution)/shard_map/ppermute | solution.py:18
  110.6 3.8 %copy-start.2 = (bf16[4096,2]{0,1:T(2,128)(2,1)}, bf16[4096,2]{0,1:T(2,128)(2,1)S(1)}, u32[]{:S(2)}) copy-start(bf16[4096,2]{0,1:T(2,128)(2,1)S(1)} %collective-permute-done.1) | copy-start | bytes 49156
  110.6 3.2 %collective-permute-start.2 = (bf16[4096,2]{0,1:T(2,128)(2,1)S(1)}, bf16[4096,2]{0,1:T(2,128)(2,1)S(1)}, u32[]{:S(2)}, u32[]{:S(2)}) collective-permute-start(bf16[4096,2]{0,1:T(2,128)(2,1)S(1)} %collective-permute-done.1), channel_id=1, source_target_pairs={{0,32},{32,64},{64,96},{96,128},{128,160},{160,192},{192,224},{224... | collective-permute-start | bytes 49160 | tf_op jit(solution)/shard_map/ppermute | solution.py:16
  110.9 3.5 %copy-start.3 = (bf16[4096,2]{0,1:T(2,128)(2,1)}, bf16[4096,2]{0,1:T(2,128)(2,1)S(1)}, u32[]{:S(2)}) copy-start(bf16[4096,2]{0,1:T(2,128)(2,1)S(1)} %collective-permute-done.5) | copy-start | bytes 49156
  110.9 3.5 %collective-permute-start.6 = (bf16[4096,2]{0,1:T(2,128)(2,1)S(1)}, bf16[4096,2]{0,1:T(2,128)(2,1)S(1)}, u32[]{:S(2)}, u32[]{:S(2)}) collective-permute-start(bf16[4096,2]{0,1:T(2,128)(2,1)S(1)} %collective-permute-done.5), channel_id=1, source_target_pairs={{0,224},{32,0},{64,32},{96,64},{128,96},{160,128},{192,160},{224,1... | collective-permute-start | bytes 49160 | tf_op jit(solution)/shard_map/ppermute | solution.py:18
  113.7 0.7 copy-start.4
  113.7 3.3 %collective-permute-start.3 = (bf16[4096,2]{0,1:T(2,128)(2,1)S(1)}, bf16[4096,2]{0,1:T(2,128)(2,1)}, u32[]{:S(2)}, u32[]{:S(2)}) collective-permute-start(bf16[4096,2]{0,1:T(2,128)(2,1)S(1)} %collective-permute-done.2), channel_id=1, source_target_pairs={{0,32},{32,64},{64,96},{96,128},{128,160},{160,192},{192,224},{224... | collective-permute-start | bytes 49160 | tf_op jit(solution)/shard_map/ppermute | solution.py:16
  114.4 0.6 copy-start.5
